TPU v7x, 32 devices: a whole 2x2x4 slice. The times are simulated.
32 devices in a mesh: site: 2 (over core), replica: 4 (over z), model: 4 (over y, x).
Axes of the slice: x: 2, y: 2, z: 4, core: 2. Of those that a mesh axis runs over, the one named last changes fastest.
Arguments:
- partial_query: bfloat16 [8, 1024, 1024], P(('site', 'replica'), None, 'model'), parts along dimension 0, may hold values from -4 to 4
- partial_key: bfloat16 [8, 1024, 1024], P(('site', 'replica'), None, 'model'), parts along dimension 0, may hold values from -4 to 4
- partial_value: bfloat16 [8, 1024, 1024], P(('site', 'replica'), None, 'model'), parts along dimension 0, may hold values from -4 to 4
- partial_mixed: bfloat16 [8, 1024, 1024], P(('site', 'replica'), 'model'), parts along dimension 0, may hold values from -4 to 4
- partial_norm: bfloat16 [8, 1024], P(('site', 'replica')), parts along dimension 0, may hold values from -8 to 8
- master_query: float32 [2048, 1024], P(('site', 'replica'), 'model'), parts along dimension 0, may hold values from -0.1875 to 0.1875
- master_key: float32 [2048, 1024], P(('site', 'replica'), 'model'), parts along dimension 0, may hold values from -0.1875 to 0.1875
- master_value: float32 [2048, 1024], P(('site', 'replica'), 'model'), parts along dimension 0, may hold values from -0.1875 to 0.1875
- master_mixed: float32 [2048, 1024], P(('site', 'model'), 'replica'), parts along dimension 0, may hold values from -0.1875 to 0.1875
- master_norm: float32 [2048], P(('site', 'replica')), parts along dimension 0, may hold values from 0.25 to 1.75
- memory_query: float32 [2048, 1024], P(('site', 'replica'), 'model'), parts along dimension 0, may hold values from 0.05 to 0.8
- memory_key: float32 [2048, 1024], P(('site', 'replica'), 'model'), parts along dimension 0, may hold values from 0.05 to 0.8
- memory_value: float32 [2048, 1024], P(('site', 'replica'), 'model'), parts along dimension 0, may hold values from 0.05 to 0.8
- memory_mixed: float32 [2048, 1024], P(('site', 'model'), 'replica'), parts along dimension 0, may hold values from 0.05 to 0.8
- memory_norm: float32 [2048], P(('site', 'replica')), parts along dimension 0, may hold values from 0.05 to 0.8
Outputs:
- compute_query: bfloat16 [2048, 1024], P('site', 'model'), parts along dimension 0
- compute_key: bfloat16 [2048, 1024], P('site', 'model'), parts along dimension 0
- compute_value: bfloat16 [2048, 1024], P('site', 'model'), parts along dimension 0
- compute_mixed: bfloat16 [2048, 1024], P(('site', 'model')), parts along dimension 0
- compute_norm: bfloat16 [2048], P('site'), parts along dimension 0
- stepped_query: float32 [2048, 1024], P(('site', 'replica'), 'model'), parts along dimension 0
- stepped_key: float32 [2048, 1024], P(('site', 'replica'), 'model'), parts along dimension 0
- stepped_value: float32 [2048, 1024], P(('site', 'replica'), 'model'), parts along dimension 0
- stepped_mixed: float32 [2048, 1024], P(('site', 'model'), 'replica'), parts along dimension 0
- stepped_norm: float32 [2048], P(('site', 'replica')), parts along dimension 0
- state_new_query: float32 [2048, 1024], P(('site', 'replica'), 'model'), parts along dimension 0
- state_new_key: float32 [2048, 1024], P(('site', 'replica'), 'model'), parts along dimension 0
- state_new_value: float32 [2048, 1024], P(('site', 'replica'), 'model'), parts along dimension 0
- state_new_mixed: float32 [2048, 1024], P(('site', 'model'), 'replica'), parts along dimension 0
- state_new_norm: float32 [2048], P(('site', 'replica')), parts along dimension 0
There are 2 independent parts, one for each index of `site`. A program takes and returns all parts, laid end to end along the dimension named above; each array names one. Nothing has to cross between parts.
All inputs are finite; a program needn't handle non-finite values.
Results may differ from a plain program's by a relative error of at most 0.001.
Values may be sent and summed in bfloat16 or wider, within the bound.
A program may use at most 64 MiB of HBM per device.

v0:
```python
import jax
import jax.numpy as jnp
from jax import lax
from jax.sharding import PartitionSpec as P

learn_rate = 0.05
hold_rate = 0.7


def body(
    partial_query,
    partial_key,
    partial_value,
    partial_mixed,
    partial_norm,
    master_query,
    master_key,
    master_value,
    master_mixed,
    master_norm,
    memory_query,
    memory_key,
    memory_value,
    memory_mixed,
    memory_norm,
):
    mean_query, mean_key, mean_value, mean_mixed = (
        lax.psum_scatter(
            partial_query[0].astype(jnp.float32), "replica", scatter_dimension=0, tiled=True
        ),
        lax.psum_scatter(
            partial_key[0].astype(jnp.float32), "replica", scatter_dimension=0, tiled=True
        ),
        lax.psum_scatter(
            partial_value[0].astype(jnp.float32), "replica", scatter_dimension=0, tiled=True
        ),
        lax.psum_scatter(
            partial_mixed[0].astype(jnp.float32), "replica", scatter_dimension=1, tiled=True
        ),
    )
    whole_norm = lax.psum(partial_norm[0].astype(jnp.float32), "replica")
    place = lax.axis_index("replica")
    mean_norm = lax.dynamic_slice_in_dim(
        whole_norm, place * master_norm.shape[0], master_norm.shape[0]
    )
    mean_rate = lax.axis_size("replica") ** (-0.5)
    mean_query = mean_query * mean_rate
    mean_key = mean_key * mean_rate
    mean_value = mean_value * mean_rate
    mean_mixed = mean_mixed * mean_rate
    mean_norm = mean_norm * mean_rate
    state_new_query = hold_rate * memory_query + (1.0 - hold_rate) * mean_query * mean_query
    stepped_query = master_query - learn_rate * mean_query * lax.rsqrt(state_new_query + 1e-06)
    state_new_key = hold_rate * memory_key + (1.0 - hold_rate) * mean_key * mean_key
    stepped_key = master_key - learn_rate * mean_key * lax.rsqrt(state_new_key + 1e-06)
    state_new_value = hold_rate * memory_value + (1.0 - hold_rate) * mean_value * mean_value
    stepped_value = master_value - learn_rate * mean_value * lax.rsqrt(state_new_value + 1e-06)
    state_new_mixed = hold_rate * memory_mixed + (1.0 - hold_rate) * mean_mixed * mean_mixed
    stepped_mixed = master_mixed - learn_rate * mean_mixed * lax.rsqrt(state_new_mixed + 1e-06)
    state_new_norm = hold_rate * memory_norm + (1.0 - hold_rate) * mean_norm * mean_norm
    stepped_norm = master_norm - learn_rate * mean_norm * lax.rsqrt(state_new_norm + 1e-06)
    compute_query, compute_key, compute_value, compute_mixed, compute_norm = (
        lax.all_gather(stepped_query.astype(jnp.bfloat16), "replica", axis=0, tiled=True),
        lax.all_gather(stepped_key.astype(jnp.bfloat16), "replica", axis=0, tiled=True),
        lax.all_gather(stepped_value.astype(jnp.bfloat16), "replica", axis=0, tiled=True),
        lax.all_gather(stepped_mixed.astype(jnp.bfloat16), "replica", axis=1, tiled=True),
        lax.all_gather(stepped_norm.astype(jnp.bfloat16), "replica", axis=0, tiled=True),
    )
    return (
        compute_query,
        compute_key,
        compute_value,
        compute_mixed,
        compute_norm,
        stepped_query,
        stepped_key,
        stepped_value,
        stepped_mixed,
        stepped_norm,
        state_new_query,
        state_new_key,
        state_new_value,
        state_new_mixed,
        state_new_norm,
    )


def solution(mesh):
    placed = (
        P(("site", "replica"), None, "model"),
        P(("site", "replica"), None, "model"),
        P(("site", "replica"), None, "model"),
        P(("site", "replica"), "model", None),
        P(("site", "replica"), None),
        P(("site", "replica"), "model"),
        P(("site", "replica"), "model"),
        P(("site", "replica"), "model"),
        P(("site", "model"), "replica"),
        P(("site", "replica")),
        P(("site", "replica"), "model"),
        P(("site", "replica"), "model"),
        P(("site", "replica"), "model"),
        P(("site", "model"), "replica"),
        P(("site", "replica")),
    )
    return jax.shard_map(
        body,
        mesh=mesh,
        in_specs=placed,
        out_specs=(
            P("site", "model"),
            P("site", "model"),
            P("site", "model"),
            P(("site", "model"), None),
            P("site"),
            P(("site", "replica"), "model"),
            P(("site", "replica"), "model"),
            P(("site", "replica"), "model"),
            P(("site", "model"), "replica"),
            P(("site", "replica")),
            P(("site", "replica"), "model"),
            P(("site", "replica"), "model"),
            P(("site", "replica"), "model"),
            P(("site", "model"), "replica"),
            P(("site", "replica")),
        ),
        check_vma=False,
    )
```

profile of v0, /device:TPU:0, one launch (start us, length us, event | category | flops | bytes accessed | tf_op | source)
XLA Modules:
  0.0 167.0 jit_solution(16219474354706718690)
XLA Ops:
  7.2 2.1 %bitcast_convert_fusion.3 = f32[1024,256]{1,0:T(8,128)} fusion(bf16[1,1024,256]{2,1,0:T(8,128)(2,1)} %param.15), kind=kLoop, calls=%fused_computation.3 | loop fusion | flops 262144 | bytes 1572864 | tf_op jit(solution)/shard_map/convert_element_type | solution.py:29
  9.4 1.0 copy-done
  10.4 1.1 bitcast_convert_fusion.2
  11.5 1.0 copy-done.1
  12.5 1.0 bitcast_convert_fusion.1
  13.6 1.0 copy-done.2
  14.6 1.1 bitcast_convert_fusion
  16.4 14.0 %psum.7 = f32[1024]{0:T(1024)S(1)} all-reduce(f32[1024]{0:T(1024)S(1)} %bitcast.15), channel_id=1, replica_groups=mesh['site'=2,'replica'=4,'model'=4] {'replica'}, use_global_device_ids=true, to_apply=%region_4.0 | all-reduce | flops 1024 | bytes 8192 | tf_op jit(solution)/shard_map/psum | solution.py:41
  31.0 7.7 %all-gather = bf16[4,1,256]{2,1,0:T(2,128)(2,1)S(1)} all-gather(bf16[1,1,256]{2,1,0:T(2,128)(2,1)S(1)} %reshape.45), channel_id=1, replica_groups=mesh['site'=2,'replica'=4,'model'=4] {'replica'}, dimensions={0}, use_global_device_ids=true | all-gather | bytes 2560 | tf_op jit(solution)/shard_map/all_gather | solution.py:67
  39.3 1.3 reduce-scatter.5.cloned.1.call-done
  40.7 1.8 %fusion.4 = (bf16[256,256]{1,0:T(8,128)(2,1)S(1)}, f32[256,256]{1,0:T(8,128)}, f32[256,256]{1,0:T(8,128)}) fusion(f32[256,256]{1,0:T(8,128)S(1)} %copy-done.3, f32[256,256]{1,0:T(8,128)} %reduce-scatter.5.cloned.1.call-done, f32[256,256]{1,0:T(8,128)S(1)} %copy-done.4), kind=kLoop, calls=%fused_computation.18 | loop fusion | flops 655360 | bytes 1441792 | tf_op jit(solution)/shard_map/convert_element_type | solution.py:63
  42.5 19.5 %all_gather.15 = bf16[1024,256]{1,0:T(8,128)(2,1)S(1)} all-gather(bf16[256,256]{1,0:T(8,128)(2,1)S(1)} %get-tuple-element.27), channel_id=1, replica_groups=mesh['site'=2,'replica'=4,'model'=4] {'replica'}, dimensions={0}, use_global_device_ids=true | all-gather | bytes 655360 | tf_op jit(solution)/shard_map/all_gather | solution.py:63
  62.0 10.9 %reduce-scatter.7.cloned.1.call-done = f32[256,256]{1,0:T(8,128)} async-done(((f32[1024,256]{1,0:T(8,128)}), f32[256,256]{1,0:T(8,128)}) %reduce-scatter.7.cloned.1.call-update) | async-done | bytes 262160 | tf_op jit(solution)/shard_map/reduce_scatter | solution.py:31
  72.9 1.8 %fusion.3 = (bf16[256,256]{1,0:T(8,128)(2,1)S(1)}, f32[256,256]{1,0:T(8,128)}, f32[256,256]{1,0:T(8,128)}) fusion(f32[256,256]{1,0:T(8,128)S(1)} %copy-done.5, f32[256,256]{1,0:T(8,128)} %reduce-scatter.7.cloned.1.call-done, f32[256,256]{1,0:T(8,128)S(1)} %copy-done.6), kind=kLoop, calls=%fused_computation.17 | loop fusion | flops 655360 | bytes 1441792 | tf_op jit(solution)/shard_map/convert_element_type | solution.py:64
  74.7 19.7 %all_gather.16 = bf16[1024,256]{1,0:T(8,128)(2,1)S(1)} all-gather(bf16[256,256]{1,0:T(8,128)(2,1)S(1)} %get-tuple-element.24), channel_id=1, replica_groups=mesh['site'=2,'replica'=4,'model'=4] {'replica'}, dimensions={0}, use_global_device_ids=true | all-gather | bytes 655360 | tf_op jit(solution)/shard_map/all_gather | solution.py:64
  94.4 12.1 %reduce-scatter.9.cloned.1.call-done = f32[256,256]{1,0:T(8,128)} async-done(((f32[1024,256]{1,0:T(8,128)}), f32[256,256]{1,0:T(8,128)}) %reduce-scatter.9.cloned.1.call-update) | async-done | bytes 262160 | tf_op jit(solution)/shard_map/reduce_scatter | solution.py:34
  106.5 1.8 %fusion.2 = (bf16[256,256]{1,0:T(8,128)(2,1)S(1)}, f32[256,256]{1,0:T(8,128)}, f32[256,256]{1,0:T(8,128)}) fusion(f32[256,256]{1,0:T(8,128)S(1)} %copy-done.7, f32[256,256]{1,0:T(8,128)} %reduce-scatter.9.cloned.1.call-done, f32[256,256]{1,0:T(8,128)S(1)} %copy-done.8), kind=kLoop, calls=%fused_computation.16 | loop fusion | flops 655360 | bytes 1441792 | tf_op jit(solution)/shard_map/convert_element_type | solution.py:65
  108.4 19.6 %all_gather.17 = bf16[1024,256]{1,0:T(8,128)(2,1)S(1)} all-gather(bf16[256,256]{1,0:T(8,128)(2,1)S(1)} %get-tuple-element.21), channel_id=1, replica_groups=mesh['site'=2,'replica'=4,'model'=4] {'replica'}, dimensions={0}, use_global_device_ids=true | all-gather | bytes 655360 | tf_op jit(solution)/shard_map/all_gather | solution.py:65
  128.0 11.8 %reduce-scatter.11.cloned.1.call-done = f32[256,256]{1,0:T(8,128)} async-done(((f32[256,1024]{1,0:T(8,128)}), f32[256,256]{1,0:T(8,128)}) %reduce-scatter.11.cloned.1.call-update) | async-done | bytes 262160 | tf_op jit(solution)/shard_map/reduce_scatter | solution.py:37
  139.8 1.8 %fusion.1 = (bf16[256,256]{1,0:T(8,128)(2,1)S(1)}, f32[256,256]{1,0:T(8,128)}, f32[256,256]{1,0:T(8,128)}) fusion(f32[256,256]{1,0:T(8,128)S(1)} %copy-done.9, f32[256,256]{1,0:T(8,128)} %reduce-scatter.11.cloned.1.call-done, f32[256,256]{1,0:T(8,128)S(1)} %copy-done.10), kind=kLoop, calls=%fused_computation.15 | loop fusion | flops 655360 | bytes 1441792 | tf_op jit(solution)/shard_map/convert_element_type | solution.py:66
  141.6 15.7 %all_gather.18 = bf16[256,1024]{1,0:T(8,128)(2,1)S(1)} all-gather(bf16[256,256]{1,0:T(8,128)(2,1)S(1)} %get-tuple-element.18), channel_id=1, replica_groups=mesh['site'=2,'replica'=4,'model'=4] {'replica'}, dimensions={1}, use_global_device_ids=true | all-gather | bytes 655360 | tf_op jit(solution)/shard_map/all_gather | solution.py:66
  157.3 0.8 copy.35
  158.9 0.8 copy.37
  159.7 0.8 copy.38
  (39 shorter events, 3.0 us)
Async XLA Ops:
  7.2 33.5 %reduce-scatter.5.cloned.1.call-start = ((), (), s32[]{:S(2)}) async-start(), calls=%async_computation.4 | async-start | bytes 1310720 | tf_op jit(solution)/shard_map/reduce_scatter | solution.py:28
  9.3 1.0 copy-start
  9.3 63.6 %reduce-scatter.7.cloned.1.call-start = ((), (), s32[]{:S(2)}) async-start(), calls=%async_computation.5 | async-start | bytes 1310720 | tf_op jit(solution)/shard_map/reduce_scatter | solution.py:31
  11.4 1.0 copy-start.1
  11.5 95.1 %reduce-scatter.9.cloned.1.call-start = ((), (), s32[]{:S(2)}) async-start(), calls=%async_computation.6 | async-start | bytes 1310720 | tf_op jit(solution)/shard_map/reduce_scatter | solution.py:34
  13.5 1.0 copy-start.2
  13.5 126.2 %reduce-scatter.11.cloned.1.call-start = ((), (), s32[]{:S(2)}) async-start(), calls=%async_computation.7 | async-start | bytes 1310720 | tf_op jit(solution)/shard_map/reduce_scatter | solution.py:37
  15.7 0.7 copy-start.11
  15.7 25.0 %copy-start.3 = (f32[256,256]{1,0:T(8,128)S(1)}, f32[256,256]{1,0:T(8,128)}, u32[]{:S(2)}) copy-start(f32[256,256]{1,0:T(8,128)} %param.20) | copy-start | bytes 786436
  15.7 25.0 %copy-start.4 = (f32[256,256]{1,0:T(8,128)S(1)}, f32[256,256]{1,0:T(8,128)}, u32[]{:S(2)}) copy-start(f32[256,256]{1,0:T(8,128)} %param.25) | copy-start | bytes 786436
  16.4 14.0 %copy-start.12 = (f32[256]{0:T(256)S(1)}, f32[256]{0:T(256)}, u32[]{:S(2)}) copy-start(f32[256]{0:T(256)} %param.24) | copy-start | bytes 3076
  16.4 14.0 %copy-start.13 = (f32[256]{0:T(256)S(1)}, f32[256]{0:T(256)}, u32[]{:S(2)}) copy-start(f32[256]{0:T(256)} %param.29) | copy-start | bytes 3076
  42.5 30.4 %copy-start.5 = (f32[256,256]{1,0:T(8,128)S(1)}, f32[256,256]{1,0:T(8,128)}, u32[]{:S(2)}) copy-start(f32[256,256]{1,0:T(8,128)} %param.21) | copy-start | bytes 786436
  42.5 30.4 %copy-start.6 = (f32[256,256]{1,0:T(8,128)S(1)}, f32[256,256]{1,0:T(8,128)}, u32[]{:S(2)}) copy-start(f32[256,256]{1,0:T(8,128)} %param.26) | copy-start | bytes 786436
  74.7 31.8 %copy-start.7 = (f32[256,256]{1,0:T(8,128)S(1)}, f32[256,256]{1,0:T(8,128)}, u32[]{:S(2)}) copy-start(f32[256,256]{1,0:T(8,128)} %param.22) | copy-start | bytes 786436
  74.7 31.8 %copy-start.8 = (f32[256,256]{1,0:T(8,128)S(1)}, f32[256,256]{1,0:T(8,128)}, u32[]{:S(2)}) copy-start(f32[256,256]{1,0:T(8,128)} %param.27) | copy-start | bytes 786436
  108.4 31.4 %copy-start.9 = (f32[256,256]{1,0:T(8,128)S(1)}, f32[256,256]{1,0:T(8,128)}, u32[]{:S(2)}) copy-start(f32[256,256]{1,0:T(8,128)} %param.23) | copy-start | bytes 786436
  108.4 31.4 %copy-start.10 = (f32[256,256]{1,0:T(8,128)S(1)}, f32[256,256]{1,0:T(8,128)}, u32[]{:S(2)}) copy-start(f32[256,256]{1,0:T(8,128)} %param.28) | copy-start | bytes 786436
Sparse Core Ops, SparseCore 0:
  10.3 30.3 reduce-scatter.4
  42.9 29.9 reduce-scatter.6
  75.2 31.2 reduce-scatter.8
  108.7 31.0 reduce-scatter.10
where the time goes:
time: 168 us; the launch traced here: 167 us
  blocking collectives  96.2 us (57%)
  waiting for transfers between devices  36.2 us (22%)
  between operations  13.8 us (8%)
  other arithmetic  13.3 us (8%)
  local copies, waits for them, and re-layouts  7.35 us (4%)
    all_gather x1, blocking collectives, body(): lax.all_gather(stepped_key.astype(jnp.bfloat16), 'replica', axis=0, tiled...  19.7 us
    all_gather x1, blocking collectives, body(): lax.all_gather(stepped_value.astype(jnp.bfloat16), 'replica', axis=0, til...  19.6 us
    all_gather x1, blocking collectives, body(): lax.all_gather(stepped_query.astype(jnp.bfloat16), 'replica', axis=0, til...  19.5 us
    all_gather x1, blocking collectives, body(): lax.all_gather(stepped_mixed.astype(jnp.bfloat16), 'replica', axis=1, til...  15.7 us
    psum x1, blocking collectives, body(): whole_norm = lax.psum(partial_norm[0].astype(jnp.float32), 'replica')  14 us
    reduce_scatter x1, waiting for transfers between devices, body(): lax.psum_scatter(partial_value[0].astype(jnp.float32), 'replica', scatter...  12.1 us
    reduce_scatter x1, waiting for transfers between devices, body(): lax.psum_scatter(partial_mixed[0].astype(jnp.float32), 'replica', scatter...  11.8 us
    reduce_scatter x1, waiting for transfers between devices, body(): lax.psum_scatter(partial_key[0].astype(jnp.float32), 'replica', scatter_d...  10.9 us
  transfers between devices with their start and end apart: 4, of which 4 were waited for; matrix products, arithmetic and copies ran while one was open for 6% of the time, Pallas kernels for 0%

commit v1 on v0

v1 whole, which is shorter than its diff:
```python
import functools

import jax
import jax.numpy as jnp
from jax import lax
from jax.experimental import pallas as pl
from jax.experimental.pallas import tpu as pltpu
from jax.sharding import PartitionSpec as P

learn_rate = 0.05
hold_rate = 0.7
HALVES = 2
MESH = pl.DeviceIdType.MESH
LINK = jnp.bfloat16
MATRICES = 4
LIMIT = 4.0
TOP = 120.0


def update(mean, master, memory):
    state = hold_rate * memory + (1.0 - hold_rate) * mean * mean
    return master - learn_rate * mean * lax.rsqrt(state + 1e-06), state


def encode(value, gain):
    size = jnp.exp2(jnp.abs(value) * gain - TOP)
    return jnp.where(value < 0, -size, size).astype(LINK)


def decode(code, step):
    code = code.astype(jnp.float32)
    size = (jnp.log2(jnp.abs(code)) + TOP) * step
    return jnp.where(code < 0, -size, size)


def kernel(n, halves, *refs):
    T = MATRICES
    (partial, master, memory) = refs[0:T], refs[T : 2 * T], refs[2 * T : 3 * T]
    norm_in = refs[3 * T]
    at = 3 * T + 1
    compute, stepped, state = refs[at : at + T], refs[at + T : at + 2 * T], refs[at + 2 * T : at + 3 * T]
    compute_norm, stepped_norm, state_norm = refs[at + 3 * T : at + 3 * T + 3]
    (
        tall, wide, master_v, memory_v, send_v, recv_v, acc, step_v, state_v, tall_g, wide_g, norm_v,
        load_sem, rs_send, rs_recv, ag_send, ag_recv, norm_send, norm_recv, out_sem, gather_sem,
    ) = refs[at + 3 * T + 3 :]
    me = lax.axis_index("replica")
    rows, cols = master[0].shape
    part = rows // halves
    rate = n ** (-0.5)

    def spot(plane, planes_wide, t, s, h):
        if t < T - 1:
            top = pl.multiple_of(s * rows + h * part, part)
            return plane.at[t, pl.ds(top, part), :]
        return planes_wide.at[pl.ds(h * part, part), pl.ds(pl.multiple_of(s * cols, cols), cols)]

    loads = []
    for t in range(T):
        loads.append(
            (
                pltpu.make_async_copy(partial[t], tall.at[t] if t < T - 1 else wide, load_sem.at[0, t]),
                pltpu.make_async_copy(master[t], master_v.at[t], load_sem.at[1, t]),
                pltpu.make_async_copy(memory[t], memory_v.at[t], load_sem.at[2, t]),
            )
        )
    for t in range(T):
        loads[t][0].start()
    for t in range(T):
        loads[t][1].start()
        loads[t][2].start()

    barrier = pltpu.get_barrier_semaphore()
    for d in range(1, n):
        pl.semaphore_signal(
            barrier, inc=1, device_id={"replica": lax.rem(me + d, n)}, device_id_type=MESH
        )
    pl.semaphore_wait(barrier, n - 1)

    def norm_copy(d):
        return pltpu.make_async_remote_copy(
            src_ref=norm_in,
            dst_ref=norm_v.at[d - 1],
            send_sem=norm_send.at[d - 1],
            recv_sem=norm_recv.at[d - 1],
            device_id={"replica": lax.rem(me + d, n)},
            device_id_type=MESH,
        )

    def sum_copy(way, c, s, source=None):
        return pltpu.make_async_remote_copy(
            src_ref=send_v.at[way, c, s] if source is None else source,
            dst_ref=recv_v.at[way, c, s],
            send_sem=rs_send.at[way, c, s],
            recv_sem=rs_recv.at[way, c, s],
            device_id={"replica": me + 1 - 2 * way},
            device_id_type=MESH,
        )

    def share_copy(way, c, s):
        t, h = c // halves, c % halves
        place = spot(tall_g, wide_g, t, s, h)
        return pltpu.make_async_remote_copy(
            src_ref=place,
            dst_ref=place,
            send_sem=ag_send.at[way, c, s],
            recv_sem=ag_recv.at[way, c, s],
            device_id={"replica": me + 1 - 2 * way},
            device_id_type=MESH,
        )

    def terms(way):
        return me + 1 if way == 0 else n - me

    def gain(way):
        return (2 * TOP / LIMIT) / terms(way).astype(jnp.float32)

    def arrived(way, c, s):
        step = (terms(way) - 1).astype(jnp.float32) * (LIMIT / (2 * TOP))
        code = recv_v[way, c, s]
        return jnp.where(terms(way) == 2, code.astype(jnp.float32), decode(code, step))

    def behind(way):
        return me > 0 if way == 0 else me < n - 1

    def ahead(way, d):
        return me + d < n if way == 0 else me - d >= 0

    def sums(c):
        t, h = c // halves, c % halves
        if h == 0:
            loads[t][0].wait()
        for d in range(n - 1, 0, -1):
            for way in range(2):
                s = me + d if way == 0 else me - d

                @pl.when(jnp.logical_and(ahead(way, d), jnp.logical_not(behind(way))))
                def _():
                    sum_copy(way, c, s, spot(tall, wide, t, s, h)).start()

                @pl.when(jnp.logical_and(ahead(way, d), behind(way)))
                def _():
                    own = spot(tall, wide, t, s, h)[...].astype(jnp.float32)
                    sum_copy(way, c, s).wait_recv()
                    send_v[way, c, s] = encode(own + arrived(way, c, s), gain(way))
                    sum_copy(way, c, s).start()

    def finish(c):
        t, h = c // halves, c % halves
        if h == 0:
            loads[t][1].wait()
            loads[t][2].wait()
        acc[...] = spot(tall, wide, t, me, h)[...].astype(jnp.float32)
        for way in range(2):

            @pl.when(behind(way))
            def _():
                sum_copy(way, c, me).wait_recv()
                acc[...] += arrived(way, c, me)

        band = pl.ds(h * part, part)
        new, held = update(acc[...] * rate, master_v[t, band, :], memory_v[t, band, :])
        spot(tall_g, wide_g, t, me, h)[...] = new.astype(jnp.bfloat16)
        for way in range(2):

            @pl.when(ahead(way, 1))
            def _():
                share_copy(way, c, me).start()

        step_v[t, band, :] = new
        state_v[t, band, :] = held
        if h == halves - 1:
            pltpu.make_async_copy(step_v.at[t], stepped[t], out_sem.at[0, t]).start()
            pltpu.make_async_copy(state_v.at[t], state[t], out_sem.at[1, t]).start()

    def gathered_copy(t):
        return pltpu.make_async_copy(tall_g.at[t] if t < T - 1 else wide_g, compute[t], gather_sem.at[t])

    def forward(c):
        t, h = c // halves, c % halves
        for d in range(1, n):
            for way in range(2):
                s = me - d if way == 0 else me + d
                there = s >= 0 if way == 0 else s < n

                @pl.when(there)
                def _():
                    share_copy(way, c, s).wait_recv()

                @pl.when(jnp.logical_and(there, ahead(way, 1)))
                def _():
                    share_copy(way, c, s).start()

        if h == halves - 1:
            gathered_copy(t).start()

    count = T * halves
    for step in range(count + 2):
        if step < count:
            sums(step)
        if step == 0:
            for d in range(1, n):
                norm_copy(d).start()
        if 1 <= step <= count:
            finish(step - 1)
        if step >= 2:
            forward(step - 2)

    whole = norm_in.shape[1] - 2 * cols
    for d in range(1, n):
        norm_copy(d).wait()
    mean_norm = norm_in[:, :whole]
    for d in range(1, n):
        mean_norm = mean_norm + norm_v[d - 1][:, :whole]
    mean_norm = mean_norm * rate
    for s in range(n):
        mean_s = mean_norm[:, s * cols : (s + 1) * cols]

        @pl.when(me == s)
        def _():
            new, held = update(mean_s, norm_in[:, whole : whole + cols], norm_in[:, whole + cols :])
            stepped_norm[...] = new
            state_norm[...] = held
            compute_norm[:, s * cols : (s + 1) * cols] = new.astype(jnp.bfloat16)

        @pl.when(me != s)
        def _():
            slot = lax.rem(me - s + n, n) - 1
            new, held = update(
                mean_s, norm_v[slot, :, whole : whole + cols], norm_v[slot, :, whole + cols :]
            )
            compute_norm[:, s * cols : (s + 1) * cols] = new.astype(jnp.bfloat16)

    for c in range(count):
        for d in range(1, n):
            for way in range(2):

                @pl.when(ahead(way, d))
                def _():
                    sum_copy(way, c, me + d if way == 0 else me - d).wait_send()

        for d in range(n):
            for way in range(2):
                s = me - d if way == 0 else me + d

                @pl.when(jnp.logical_and(s >= 0 if way == 0 else s < n, ahead(way, 1)))
                def _():
                    share_copy(way, c, s).wait_send()

    for t in range(T):
        pltpu.make_async_copy(step_v.at[t], stepped[t], out_sem.at[0, t]).wait()
        pltpu.make_async_copy(state_v.at[t], state[t], out_sem.at[1, t]).wait()
        gathered_copy(t).wait()


def line(n, partials, masters, memories, partial_norm, master_norm, memory_norm):
    T, halves = MATRICES, HALVES
    rows, cols = masters[0].shape
    part = rows // halves
    count = T * halves
    whole = partial_norm.shape[1]
    norm_in = jnp.concatenate(
        [partial_norm.astype(jnp.float32), master_norm[None], memory_norm[None]], axis=1
    )
    f32, bf16 = jnp.float32, jnp.bfloat16
    anywhere = pl.BlockSpec(memory_space=pl.ANY)
    inside = pl.BlockSpec(memory_space=pltpu.VMEM)
    share = jax.ShapeDtypeStruct((rows, cols), f32)
    dma = pltpu.SemaphoreType.DMA
    out = pl.pallas_call(
        functools.partial(kernel, n, halves),
        out_shape=[jax.ShapeDtypeStruct(p.shape, bf16) for p in partials]
        + [share] * (2 * T)
        + [jax.ShapeDtypeStruct((1, whole), bf16)]
        + [jax.ShapeDtypeStruct((1, cols), f32)] * 2,
        in_specs=[anywhere] * (3 * T) + [inside],
        out_specs=[anywhere] * (3 * T) + [inside] * 3,
        scratch_shapes=[
            pltpu.VMEM((T - 1, n * rows, cols), bf16),
            pltpu.VMEM((rows, n * cols), bf16),
            pltpu.VMEM((T, rows, cols), f32),
            pltpu.VMEM((T, rows, cols), f32),
            pltpu.VMEM((2, count, n, part, cols), LINK),
            pltpu.VMEM((2, count, n, part, cols), LINK),
            pltpu.VMEM((part, cols), f32),
            pltpu.VMEM((T, rows, cols), f32),
            pltpu.VMEM((T, rows, cols), f32),
            pltpu.VMEM((T - 1, n * rows, cols), bf16),
            pltpu.VMEM((rows, n * cols), bf16),
            pltpu.VMEM((n - 1, 1, whole + 2 * cols), f32),
            dma((3, T)),
            dma((2, count, n)),
            dma((2, count, n)),
            dma((2, count, n)),
            dma((2, count, n)),
            dma((n - 1,)),
            dma((n - 1,)),
            dma((2, T)),
            dma((T,)),
        ],
        compiler_params=pltpu.CompilerParams(collective_id=0, has_side_effects=True),
        name="line_step",
    )(*partials, *masters, *memories, norm_in)
    compute, stepped, state = out[:T], out[T : 2 * T], out[2 * T : 3 * T]
    compute_norm, stepped_norm, state_norm = out[3 * T :]
    return (*compute, compute_norm[0], *stepped, stepped_norm[0], *state, state_norm[0])


def plain(n, partials, masters, memories, partial_norm, master_norm, memory_norm):
    rate = n ** (-0.5)
    axes = (0, 0, 0, 1)
    compute, stepped, state = [], [], []
    for p, master, memory, axis in zip(partials, masters, memories, axes):
        total = lax.psum_scatter(
            p.astype(jnp.float32), "replica", scatter_dimension=axis, tiled=True
        )
        new, held = update(total * rate, master, memory)
        stepped.append(new)
        state.append(held)
    whole = lax.psum(partial_norm[0].astype(jnp.float32), "replica")
    size = master_norm.shape[0]
    mean = lax.dynamic_slice_in_dim(whole, lax.axis_index("replica") * size, size) * rate
    new, held = update(mean, master_norm, memory_norm)
    stepped.append(new)
    state.append(held)
    for new, axis in zip(stepped, axes + (0,)):
        compute.append(lax.all_gather(new.astype(jnp.bfloat16), "replica", axis=axis, tiled=True))
    return (*compute, *stepped, *state)


def body(*args):
    partials = [p[0] for p in args[:4]]
    partial_norm = args[4]
    masters, master_norm = args[5:9], args[9]
    memories, memory_norm = args[10:14], args[14]
    n = lax.axis_size("replica")
    shapes = {m.shape for m in masters}
    rows, cols = masters[0].shape
    fits = (
        1 < n <= 4
        and len(shapes) == 1
        and rows % (32 * HALVES) == 0
        and cols % 128 == 0
        and master_norm.shape[0] == cols
    )
    form = line if fits else plain
    return form(n, partials, masters, memories, partial_norm, master_norm, memory_norm)


def solution(mesh):
    tall = P(("site", "replica"), None, "model")
    share, flat = P(("site", "replica"), "model"), P(("site", "replica"))
    wide = P(("site", "model"), "replica")
    shares = (share, share, share, wide, flat)
    return jax.shard_map(
        body,
        mesh=mesh,
        in_specs=(
            tall,
            tall,
            tall,
            P(("site", "replica"), "model", None),
            P(("site", "replica"), None),
            *shares,
            *shares,
        ),
        out_specs=(
            P("site", "model"),
            P("site", "model"),
            P("site", "model"),
            P(("site", "model"), None),
            P("site"),
            *shares,
            *shares,
        ),
        check_vma=False,
    )
```

time: 168 us -> 141 us (0.84)
  Pallas kernels: 0 us -> 122 us
  blocking collectives: 96.2 us -> 0 us
  waiting for transfers between devices: 36.2 us -> 0 us
  between operations: 13.8 us -> 0.7 us
  other arithmetic: 13.3 us -> 1.2 us
  local copies, waits for them, and re-layouts: 7.35 us -> 16.3 us
    pallas_call x0 -> x1, Pallas kernels: none -> 122 us  [line(): pl.pallas_call(functools.partial(kernel, n, halves), out_shape=[jax.Shape...]
    all_gather x5 -> x0, blocking collectives: 82.2 us -> none  [the longest x1 19.7 us: body(): lax.all_gather(stepped_key.astype(jnp.bfloat16), 'replica', axis=0, tiled...]
    reduce_scatter x4 -> x0, waiting for transfers between devices: 36.1 us -> none  [the longest x1 12.1 us: body(): lax.psum_scatter(partial_value[0].astype(jnp.float32), 'replica', scatter...]
    psum x1 -> x0, blocking collectives: 14 us -> none  [body(): whole_norm = lax.psum(partial_norm[0].astype(jnp.float32), 'replica')]
    convert_element_type x10 -> x1, other arithmetic: 13.3 us -> 0.01 us  [line(): partial_norm.astype(jnp.float32)]
    unnamed x34 -> x48, local copies, waits for them, and re-layouts: 7.35 us -> 16.3 us
  transfers between devices with their start and end apart: 4 -> 0, of which waited for: 4 -> 0; matrix products, arithmetic and copies ran while one was open for 6% -> 0% of each run, Pallas kernels for 0% -> 0%
where the time goes in v1:
time: 141 us; the launch traced here: 140 us
  Pallas kernels  122 us (87%)
  local copies, waits for them, and re-layouts  16.3 us (12%)
    pallas_call x1, Pallas kernels, line(): pl.pallas_call(functools.partial(kernel, n, halves), out_shape=[jax.Shape...  122 us
    unnamed x48, local copies, waits for them, and re-layouts  16.3 us

profile of v1, /device:TPU:0, one launch (start us, length us, event | category | flops | bytes accessed | tf_op | source)
XLA Modules:
  0.0 140.0 jit_solution(5028640303838735606)
XLA Ops:
  0.7 0.7 copy-done.11
  1.3 0.7 copy-done.13
  2.0 0.6 pad_maximum_fusion.refs_12_
  2.6 121.8 %line_step.1 = (bf16[1024,256]{1,0:T(8,128)(2,1)}, bf16[1024,256]{1,0:T(8,128)(2,1)}, bf16[1024,256]{1,0:T(8,128)(2,1)}, bf16[256,1024]{1,0:T(8,128)(2,1)}, f32[...) custom-call(bf16[1024,256]{1,0:T(8,128)(2,1)} %bitcast.8, ...), custom_call_target="tpu_custom_call" | custom-call | tf_op jit(solution)/shard_map/line_step/pallas_call | solution.py:270
  124.5 0.7 copy-done.12
  125.1 0.6 reduce
  125.7 1.9 %copy.44 = bf16[1024,256]{1,0:T(8,128)(2,1)} copy(bf16[1024,256]{1,0:T(8,128)(2,1)} %get-tuple-element.60) | data formatting | bytes 1048576
  127.7 0.8 copy.45
  128.4 0.4 copy-done.1
  128.9 0.8 copy.46
  129.7 0.4 copy-done
  130.1 0.8 copy.47
  131.2 0.7 copy.48
  132.3 0.7 copy.49
  133.0 0.3 copy-done.8
  133.3 0.7 copy.50
  134.0 0.3 copy-done.7
  134.3 0.7 copy.51
  135.0 0.6 copy.52
  135.6 0.7 copy.53
  136.7 0.7 copy.54
  137.7 0.7 copy.55
  138.8 0.7 copy.56
  139.5 0.6 copy.57
  (28 shorter events, 1.7 us)
Async XLA Ops:
  0.6 0.7 copy-start.11
  1.3 0.7 copy-start.13
  1.3 0.7 copy-start.14
  124.4 0.7 copy-start.12
  125.7 1.9 %copy-start.2 = (bf16[1024,256]{1,0:T(8,128)(2,1)S(1)}, bf16[1024,256]{1,0:T(8,128)(2,1)}, u32[]{:S(2)}) copy-start(bf16[1024,256]{1,0:T(8,128)(2,1)} %get-tuple-element.61) | copy-start | bytes 1572868
  127.7 1.2 copy-start.1
  128.9 1.2 copy-start
  130.1 1.1 copy-start.10
  131.2 1.0 copy-start.9
  132.2 1.0 copy-start.8
  133.3 1.0 copy-start.7
  134.3 0.7 copy-start.16
  134.3 1.3 copy-start.6
  135.6 1.0 copy-start.5
  136.7 1.0 copy-start.4
  137.7 1.0 copy-start.3
  138.8 0.7 copy-start.15

commit v2 on v1

--- a/solution.py
+++ b/solution.py
@@ -10,6 +10,8 @@
 learn_rate = 0.05
 hold_rate = 0.7
 HALVES = 2
+GAP = 1
+LEAD = 2
 MESH = pl.DeviceIdType.MESH
 LINK = jnp.bfloat16
 MATRICES = 4
@@ -41,34 +43,39 @@
     compute, stepped, state = refs[at : at + T], refs[at + T : at + 2 * T], refs[at + 2 * T : at + 3 * T]
     compute_norm, stepped_norm, state_norm = refs[at + 3 * T : at + 3 * T + 3]
     (
-        tall, wide, master_v, memory_v, send_v, recv_v, acc, step_v, state_v, tall_g, wide_g, norm_v,
-        load_sem, rs_send, rs_recv, ag_send, ag_recv, norm_send, norm_recv, out_sem, gather_sem,
+        tall, master_v, memory_v, send_v, recv_v, acc, step_v, state_v, tall_g, norm_v, load_sem,
+        held_sem, rs_send, rs_recv, ag_send, ag_recv, norm_send, norm_recv, out_sem, gather_sem,
     ) = refs[at + 3 * T + 3 :]
     me = lax.axis_index("replica")
     rows, cols = master[0].shape
     part = rows // halves
     rate = n ** (-0.5)
 
-    def spot(plane, planes_wide, t, s, h):
+    def spot(plane, c, s):
+        top = pl.multiple_of(s * rows + (c % halves) * part, part)
+        return plane.at[c // halves, pl.ds(top, part), :]
+
+    def laid(plane, whole, t, out, sem):
         if t < T - 1:
-            top = pl.multiple_of(s * rows + h * part, part)
-            return plane.at[t, pl.ds(top, part), :]
-        return planes_wide.at[pl.ds(h * part, part), pl.ds(pl.multiple_of(s * cols, cols), cols)]
-
-    loads = []
-    for t in range(T):
-        loads.append(
-            (
-                pltpu.make_async_copy(partial[t], tall.at[t] if t < T - 1 else wide, load_sem.at[0, t]),
-                pltpu.make_async_copy(master[t], master_v.at[t], load_sem.at[1, t]),
-                pltpu.make_async_copy(memory[t], memory_v.at[t], load_sem.at[2, t]),
-            )
-        )
-    for t in range(T):
-        loads[t][0].start()
-    for t in range(T):
-        loads[t][1].start()
-        loads[t][2].start()
+            pairs = [(whole, plane.at[t])]
+        else:
+            pairs = [
+                (whole.at[:, s * cols : (s + 1) * cols], plane.at[t, s * rows : (s + 1) * rows])
+                for s in range(n)
+            ]
+        return [
+            pltpu.make_async_copy(*(pair[::-1] if out else pair), sem.at[t, i])
+            for i, pair in enumerate(pairs)
+        ]
+
+    loads = [laid(tall, partial[t], t, False, load_sem) for t in range(T)]
+    held = [
+        pltpu.make_async_copy(source[t], target.at[t], held_sem.at[i, t])
+        for i, (source, target) in enumerate(((master, master_v), (memory, memory_v)))
+        for t in range(T)
+    ]
+    for copy in sum(loads, []) + held:
+        copy.start()
 
     barrier = pltpu.get_barrier_semaphore()
     for d in range(1, n):
@@ -98,8 +105,7 @@
         )
 
     def share_copy(way, c, s):
-        t, h = c // halves, c % halves
-        place = spot(tall_g, wide_g, t, s, h)
+        place = spot(tall_g, c, s)
         return pltpu.make_async_remote_copy(
             src_ref=place,
             dst_ref=place,
@@ -126,31 +132,33 @@
     def ahead(way, d):
         return me + d < n if way == 0 else me - d >= 0
 
-    def sums(c):
-        t, h = c // halves, c % halves
-        if h == 0:
-            loads[t][0].wait()
+    def either(way, d):
+        return me + d if way == 0 else me - d
+
+    def inner(c):
+        return jnp.logical_and(c >= 0, c < count)
+
+    def raw(c):
         for d in range(n - 1, 0, -1):
             for way in range(2):
-                s = me + d if way == 0 else me - d
 
                 @pl.when(jnp.logical_and(ahead(way, d), jnp.logical_not(behind(way))))
                 def _():
-                    sum_copy(way, c, s, spot(tall, wide, t, s, h)).start()
-
-                @pl.when(jnp.logical_and(ahead(way, d), behind(way)))
-                def _():
-                    own = spot(tall, wide, t, s, h)[...].astype(jnp.float32)
-                    sum_copy(way, c, s).wait_recv()
-                    send_v[way, c, s] = encode(own + arrived(way, c, s), gain(way))
-                    sum_copy(way, c, s).start()
+                    sum_copy(way, c, either(way, d), spot(tall, c, either(way, d))).start()
+
+    def sums(way, c):
+        for d in range(n - 1, 0, -1):
+            s = either(way, d)
+
+            @pl.when(jnp.logical_and(inner(c), jnp.logical_and(ahead(way, d), behind(way))))
+            def _():
+                own = spot(tall, c, s)[...].astype(jnp.float32)
+                sum_copy(way, c, s).wait_recv()
+                send_v[way, c, s] = encode(own + arrived(way, c, s), gain(way))
+                sum_copy(way, c, s).start()
 
     def finish(c):
-        t, h = c // halves, c % halves
-        if h == 0:
-            loads[t][1].wait()
-            loads[t][2].wait()
-        acc[...] = spot(tall, wide, t, me, h)[...].astype(jnp.float32)
+        acc[...] = spot(tall, c, me)[...].astype(jnp.float32)
         for way in range(2):
 
             @pl.when(behind(way))
@@ -158,9 +166,9 @@
                 sum_copy(way, c, me).wait_recv()
                 acc[...] += arrived(way, c, me)
 
-        band = pl.ds(h * part, part)
+        t, band = c // halves, pl.ds(pl.multiple_of((c % halves) * part, part), part)
         new, held = update(acc[...] * rate, master_v[t, band, :], memory_v[t, band, :])
-        spot(tall_g, wide_g, t, me, h)[...] = new.astype(jnp.bfloat16)
+        spot(tall_g, c, me)[...] = new.astype(jnp.bfloat16)
         for way in range(2):
 
             @pl.when(ahead(way, 1))
@@ -169,42 +177,68 @@
 
         step_v[t, band, :] = new
         state_v[t, band, :] = held
-        if h == halves - 1:
-            pltpu.make_async_copy(step_v.at[t], stepped[t], out_sem.at[0, t]).start()
-            pltpu.make_async_copy(state_v.at[t], state[t], out_sem.at[1, t]).start()
-
-    def gathered_copy(t):
-        return pltpu.make_async_copy(tall_g.at[t] if t < T - 1 else wide_g, compute[t], gather_sem.at[t])
-
-    def forward(c):
-        t, h = c // halves, c % halves
+
+    def forward(way, d, c, s):
+        @pl.when(jnp.logical_and(inner(c), jnp.logical_and(s >= 0, s < n)))
+        def _():
+            share_copy(way, c, s).wait_recv()
+
+            @pl.when(ahead(way, 1))
+            def _():
+                share_copy(way, c, s).start()
+
+    def depth(s):
+        return jnp.maximum(s, n - 1 - s)
+
+    def step(at, carry):
+        @pl.when(at + LEAD < count)
+        def _():
+            raw(at + LEAD)
+
+        for way in range(2):
+            sums(way, at - GAP * (terms(way) - 1))
+        c = at - GAP * depth(me)
+
+        @pl.when(inner(c))
+        def _():
+            finish(c)
+
         for d in range(1, n):
             for way in range(2):
-                s = me - d if way == 0 else me + d
-                there = s >= 0 if way == 0 else s < n
-
-                @pl.when(there)
-                def _():
-                    share_copy(way, c, s).wait_recv()
-
-                @pl.when(jnp.logical_and(there, ahead(way, 1)))
-                def _():
-                    share_copy(way, c, s).start()
-
-        if h == halves - 1:
-            gathered_copy(t).start()
+                s = either(1 - way, d)
+                forward(way, d, at - GAP * (depth(s) + d), s)
+        return carry
 
     count = T * halves
-    for step in range(count + 2):
-        if step < count:
-            sums(step)
-        if step == 0:
-            for d in range(1, n):
-                norm_copy(d).start()
-        if 1 <= step <= count:
-            finish(step - 1)
-        if step >= 2:
-            forward(step - 2)
+    for t in range(T):
+        for copy in loads[t]:
+            copy.wait()
+        for c in range(t * halves, (t + 1) * halves):
+            if c < LEAD:
+                raw(c)
+    for d in range(1, n):
+        norm_copy(d).start()
+    for copy in held:
+        copy.wait()
+
+    outs = [
+        pltpu.make_async_copy(source.at[t], target[t], out_sem.at[i, t])
+        for t in range(T)
+        for i, (source, target) in enumerate(((step_v, stepped), (state_v, state)))
+    ]
+    gathered = [laid(tall_g, compute[t], t, True, gather_sem) for t in range(T)]
+    tasks = sorted(
+        [(t * halves + halves - 1 + GAP * (n - 1), outs[2 * t : 2 * t + 2]) for t in range(T)]
+        + [(t * halves + halves - 1 + 2 * GAP * (n - 1), gathered[t]) for t in range(T)],
+        key=lambda task: task[0],
+    )
+    reached = 0
+    for last, copies in tasks:
+        if last >= reached:
+            lax.fori_loop(reached, last + 1, step, 0)
+            reached = last + 1
+        for copy in copies:
+            copy.start()
 
     whole = norm_in.shape[1] - 2 * cols
     for d in range(1, n):
@@ -231,26 +265,26 @@
             )
             compute_norm[:, s * cols : (s + 1) * cols] = new.astype(jnp.bfloat16)
 
-    for c in range(count):
-        for d in range(1, n):
-            for way in range(2):
+    def drain(c, carry):
+        for way in range(2):
+            for d in range(1, n):
 
                 @pl.when(ahead(way, d))
                 def _():
-                    sum_copy(way, c, me + d if way == 0 else me - d).wait_send()
-
-        for d in range(n):
-            for way in range(2):
-                s = me - d if way == 0 else me + d
-
-                @pl.when(jnp.logical_and(s >= 0 if way == 0 else s < n, ahead(way, 1)))
+                    sum_copy(way, c, either(way, d)).wait_send()
+
+            for d in range(n):
+                s = either(1 - way, d)
+
+                @pl.when(jnp.logical_and(jnp.logical_and(s >= 0, s < n), ahead(way, 1)))
                 def _():
                     share_copy(way, c, s).wait_send()
 
-    for t in range(T):
-        pltpu.make_async_copy(step_v.at[t], stepped[t], out_sem.at[0, t]).wait()
-        pltpu.make_async_copy(state_v.at[t], state[t], out_sem.at[1, t]).wait()
-        gathered_copy(t).wait()
+        return carry
+
+    lax.fori_loop(0, count, drain, 0)
+    for copy in outs + sum(gathered, []):
+        copy.wait()
 
 
 def line(n, partials, masters, memories, partial_norm, master_norm, memory_norm):
@@ -276,8 +310,7 @@
         in_specs=[anywhere] * (3 * T) + [inside],
         out_specs=[anywhere] * (3 * T) + [inside] * 3,
         scratch_shapes=[
-            pltpu.VMEM((T - 1, n * rows, cols), bf16),
-            pltpu.VMEM((rows, n * cols), bf16),
+            pltpu.VMEM((T, n * rows, cols), bf16),
             pltpu.VMEM((T, rows, cols), f32),
             pltpu.VMEM((T, rows, cols), f32),
             pltpu.VMEM((2, count, n, part, cols), LINK),
@@ -285,10 +318,10 @@
             pltpu.VMEM((part, cols), f32),
             pltpu.VMEM((T, rows, cols), f32),
             pltpu.VMEM((T, rows, cols), f32),
-            pltpu.VMEM((T - 1, n * rows, cols), bf16),
-            pltpu.VMEM((rows, n * cols), bf16),
+            pltpu.VMEM((T, n * rows, cols), bf16),
             pltpu.VMEM((n - 1, 1, whole + 2 * cols), f32),
-            dma((3, T)),
+            dma((T, n)),
+            dma((2, T)),
             dma((2, count, n)),
             dma((2, count, n)),
             dma((2, count, n)),
@@ -296,7 +329,7 @@
             dma((n - 1,)),
             dma((n - 1,)),
             dma((2, T)),
-            dma((T,)),
+            dma((T, n)),
         ],
         compiler_params=pltpu.CompilerParams(collective_id=0, has_side_effects=True),
         name="line_step",

time: 141 us -> 95.3 us (0.68)
  Pallas kernels: 122 us -> 76.5 us
    pallas_call x1, Pallas kernels: 122 us -> 76.5 us  [line(): pl.pallas_call(functools.partial(kernel, n, halves), out_shape=[jax.Shape...]
where the time goes in v2:
time: 95.3 us; the launch traced here: 94.7 us
  Pallas kernels  76.5 us (80%)
  local copies, waits for them, and re-layouts  16.3 us (17%)
  other arithmetic  1.2 us (1%)
    pallas_call x1, Pallas kernels, line(): pl.pallas_call(functools.partial(kernel, n, halves), out_shape=[jax.Shape...  76.5 us
    unnamed x48, local copies, waits for them, and re-layouts  16.3 us

profile of v2, /device:TPU:0, one launch (start us, length us, event | category | flops | bytes accessed | tf_op | source)
XLA Modules:
  0.0 94.7 jit_solution(12200250818720680237)
XLA Ops:
  0.7 0.7 copy-done.11
  1.3 0.7 copy-done.13
  2.0 0.6 pad_maximum_fusion.refs_12_
  2.6 76.5 %line_step.1 = (bf16[1024,256]{1,0:T(8,128)(2,1)}, bf16[1024,256]{1,0:T(8,128)(2,1)}, bf16[1024,256]{1,0:T(8,128)(2,1)}, bf16[256,1024]{1,0:T(8,128)(2,1)}, f32[...) custom-call(bf16[1024,256]{1,0:T(8,128)(2,1)} %bitcast.8, ...), custom_call_target="tpu_custom_call" | custom-call | tf_op jit(solution)/shard_map/line_step/pallas_call | solution.py:304
  79.1 0.7 copy-done.12
  79.8 0.6 reduce
  80.4 1.9 %copy.44 = bf16[1024,256]{1,0:T(8,128)(2,1)} copy(bf16[1024,256]{1,0:T(8,128)(2,1)} %get-tuple-element.60) | data formatting | bytes 1048576
  82.3 0.8 copy.45
  83.1 0.4 copy-done.1
  83.6 0.8 copy.46
  84.4 0.4 copy-done
  84.8 0.8 copy.47
  85.9 0.7 copy.48
  86.6 0.3 copy-done.9
  86.9 0.7 copy.49
  88.0 0.7 copy.50
  89.0 0.7 copy.51
  89.7 0.6 copy.52
  90.3 0.7 copy.53
  91.0 0.3 copy-done.5
  91.3 0.7 copy.54
  92.4 0.7 copy.55
  93.4 0.7 copy.56
  94.1 0.6 copy.57
  (28 shorter events, 1.7 us)
Async XLA Ops:
  0.6 0.7 copy-start.11
  1.3 0.7 copy-start.13
  1.3 0.7 copy-start.14
  79.1 0.7 copy-start.12
  80.4 1.9 %copy-start.2 = (bf16[1024,256]{1,0:T(8,128)(2,1)S(1)}, bf16[1024,256]{1,0:T(8,128)(2,1)}, u32[]{:S(2)}) copy-start(bf16[1024,256]{1,0:T(8,128)(2,1)} %get-tuple-element.61) | copy-start | bytes 1572868
  82.3 1.2 %copy-start.1 = (bf16[1024,256]{1,0:T(8,128)(2,1)S(1)}, bf16[1024,256]{1,0:T(8,128)(2,1)}, u32[]{:S(2)}) copy-start(bf16[1024,256]{1,0:T(8,128)(2,1)} %get-tuple-element.62) | copy-start | bytes 1572868
  83.6 1.2 %copy-start = (bf16[256,1024]{1,0:T(8,128)(2,1)S(1)}, bf16[256,1024]{1,0:T(8,128)(2,1)}, u32[]{:S(2)}) copy-start(bf16[256,1024]{1,0:T(8,128)(2,1)} %get-tuple-element.63) | copy-start | bytes 1572868
  84.8 1.1 %copy-start.10 = (f32[256,256]{1,0:T(8,128)S(1)}, f32[256,256]{1,0:T(8,128)}, u32[]{:S(2)}) copy-start(f32[256,256]{1,0:T(8,128)} %get-tuple-element.65) | copy-start | bytes 786436
  85.9 1.0 %copy-start.9 = (f32[256,256]{1,0:T(8,128)S(1)}, f32[256,256]{1,0:T(8,128)}, u32[]{:S(2)}) copy-start(f32[256,256]{1,0:T(8,128)} %get-tuple-element.66) | copy-start | bytes 786436
  86.9 1.0 %copy-start.8 = (f32[256,256]{1,0:T(8,128)S(1)}, f32[256,256]{1,0:T(8,128)}, u32[]{:S(2)}) copy-start(f32[256,256]{1,0:T(8,128)} %get-tuple-element.67) | copy-start | bytes 786436
  88.0 1.0 %copy-start.7 = (f32[256,256]{1,0:T(8,128)S(1)}, f32[256,256]{1,0:T(8,128)}, u32[]{:S(2)}) copy-start(f32[256,256]{1,0:T(8,128)} %get-tuple-element.68) | copy-start | bytes 786436
  89.0 0.7 copy-start.16
  89.0 1.3 %copy-start.6 = (f32[256,256]{1,0:T(8,128)S(1)}, f32[256,256]{1,0:T(8,128)}, u32[]{:S(2)}) copy-start(f32[256,256]{1,0:T(8,128)} %get-tuple-element.70) | copy-start | bytes 786436
  90.3 1.0 %copy-start.5 = (f32[256,256]{1,0:T(8,128)S(1)}, f32[256,256]{1,0:T(8,128)}, u32[]{:S(2)}) copy-start(f32[256,256]{1,0:T(8,128)} %get-tuple-element.71) | copy-start | bytes 786436
  91.3 1.0 %copy-start.4 = (f32[256,256]{1,0:T(8,128)S(1)}, f32[256,256]{1,0:T(8,128)}, u32[]{:S(2)}) copy-start(f32[256,256]{1,0:T(8,128)} %get-tuple-element.72) | copy-start | bytes 786436
  92.4 1.0 %copy-start.3 = (f32[256,256]{1,0:T(8,128)S(1)}, f32[256,256]{1,0:T(8,128)}, u32[]{:S(2)}) copy-start(f32[256,256]{1,0:T(8,128)} %get-tuple-element.73) | copy-start | bytes 786436
  93.4 0.7 copy-start.15
